TPU v7x, 32 devices: a whole 2x2x4 slice. The times are simulated.
32 devices in a mesh: mc: 8 (over z, x), mr: 4 (over y, core).
Axes of the slice: x: 2, y: 2, z: 4, core: 2. Of those that a mesh axis runs over, the one named last changes fastest.
Arguments:
- column_panel: float32 [4096, 256], P('mc', 'mr'), may hold values from -0.375 to 0.375
- diag_block: float32 [256, 256], P('mc', 'mr'), may hold values from -4.3 to 4.3, as said below
- row_panel: float32 [256, 32768], P('mc', 'mr'), may hold values from -6 to 6
- trailing: float32 [4096, 32768], P('mc', 'mr'), may hold values from -6 to 6
Outputs:
- solved_panel: float32 [4096, 256], P('mc', 'mr')
- inverse_block: float32 [256, 256], P('mc', 'mr')
- scaled_panel: float32 [256, 32768], P('mc', 'mr')
- updated: float32 [4096, 32768], P('mc', 'mr')
Inputs may be any that keep to these rules, and one draw needn't show every extreme that they name: `diag_block`: upper triangle with a diagonal of magnitude 2 to 4 and small off-diagonal entries.
All inputs are finite; a program needn't handle non-finite values.
Results may differ from a plain program's by a relative error of at most 0.00011.
Values sent between devices are 32-bit elements; how exact they have to be, the bound alone decides.
A program may use at most 128 MiB of HBM per device.

v0:
```python
import jax
import jax.numpy as jnp
from jax import lax
from jax.sharding import PartitionSpec as P


def upper_inverse(matrix):
    order = matrix.shape[0]
    upper = jnp.triu(matrix)
    pivots = jnp.diagonal(upper)
    recip = 1.0 / pivots
    strict = upper - jnp.diag(pivots)
    nilpotent = -(recip[:, None] * strict)
    identity = jnp.eye(order, dtype=matrix.dtype)
    product = identity + nilpotent
    power = nilpotent
    steps = max((order - 1).bit_length(), 1)
    for level in range(steps - 1):
        power = jnp.dot(power, power, precision=lax.Precision.HIGHEST)
        product = jnp.dot(product, identity + power, precision=lax.Precision.HIGHEST)
    return product * recip[None, :]


def shards(column_panel, diag_block, row_panel, trailing):
    block_rows = diag_block.shape[0]
    block_cols = diag_block.shape[1]
    grid_row = lax.axis_index("mc")
    grid_col = lax.axis_index("mr")
    diag_part = lax.all_gather(diag_block, "mc", axis=0, tiled=True)
    diag_whole = lax.all_gather(diag_part, "mr", axis=1, tiled=True)
    inverse = upper_inverse(diag_whole)
    own_inverse = lax.dynamic_slice_in_dim(inverse, grid_row * block_rows, block_rows, 0)
    gathered = lax.all_gather(column_panel, "mr", axis=1, tiled=True)
    column_whole = -jnp.dot(gathered, inverse, precision=lax.Precision.HIGHEST)
    piece = lax.all_gather(row_panel, "mc", axis=0, tiled=True)
    trail_sum = trailing
    trail_sum = trail_sum + jnp.dot(column_whole, piece, precision=lax.Precision.HIGHEST)
    scaled_sum = jnp.dot(own_inverse, piece, precision=lax.Precision.HIGHEST)
    solved_panel = lax.dynamic_slice_in_dim(column_whole, grid_col * block_cols, block_cols, 1)
    inverse_part = lax.dynamic_slice_in_dim(own_inverse, grid_col * block_cols, block_cols, 1)
    return (solved_panel, inverse_part, scaled_sum, trail_sum)


def solution(mesh):
    placed = (P("mc", "mr"), P("mc", "mr"), P("mc", "mr"), P("mc", "mr"))
    return jax.shard_map(
        shards,
        mesh=mesh,
        in_specs=placed,
        out_specs=(P("mc", "mr"), P("mc", "mr"), P("mc", "mr"), P("mc", "mr")),
        check_vma=False,
    )
```

profile of v0, /device:TPU:0, one launch (start us, length us, event | category | flops | bytes accessed | tf_op | source)
XLA Modules:
  0.0 172.9 jit_solution(2714709711748842154)
XLA Ops:
  7.2 0.0 copy-start.1
  7.2 0.0 all-gather.2.cloned.1.call-start
  7.2 0.7 all-gather.2.cloned.1.call-update
  7.9 33.8 %all_gather.12 = f32[256,64]{1,0:T(8,128)S(1)} all-gather(f32[32,64]{1,0:T(8,128)} %param.5), channel_id=1, replica_groups=mesh['mc'=8,'mr'=4] {'mc'}, dimensions={0}, use_global_device_ids=true | all-gather | bytes 73728 | tf_op jit(solution)/shard_map/all_gather | solution.py:29
  41.7 0.1 copy.10
  41.8 5.8 %all_gather.13 = f32[256,256]{0,1:T(8,128)S(1)} all-gather(f32[256,64]{0,1:T(8,128)S(1)} %copy.10), channel_id=1, replica_groups=mesh['mc'=8,'mr'=4] {'mr'}, dimensions={1}, use_global_device_ids=true | all-gather | bytes 327680 | tf_op jit(solution)/shard_map/all_gather | solution.py:30
  47.6 0.1 copy.11
  47.8 0.1 fusion.6
  47.9 2.3 %gather_fusion = f32[256]{0:T(256)S(1)} fusion(f32[256,256]{1,0:T(8,128)S(1)} %fusion.6, s32[256]{0:T(256)S(1)} %bitcast.27), kind=kCustom, calls=%fused_computation | custom fusion | bytes 4096 | tf_op jit(solution)/shard_map/jit(diagonal)/cond/branch_0_fun/gather | solution.py:10
  50.2 0.5 fusion.7
  50.7 0.4 fusion.19
  51.1 0.4 fusion.20
  51.5 0.4 fusion
  52.0 0.4 fusion.1
  52.4 0.4 fusion.21
  52.7 0.4 fusion.2
  53.2 0.4 fusion.22
  53.5 0.4 fusion.3
  53.9 0.4 fusion.23
  54.3 0.4 fusion.4
  54.7 0.4 convolution_add_fusion.1
  55.1 0.4 fusion.5
  55.5 0.4 convolution_multiply_fusion
  55.9 0.7 dynamic_slice.10
  56.6 0.0 copy-done.1
  56.6 7.4 %all_gather.14 = f32[512,256]{0,1:T(8,128)S(1)} all-gather(f32[512,64]{0,1:T(8,128)S(1)} %copy-done.1), channel_id=1, replica_groups=mesh['mc'=8,'mr'=4] {'mr'}, dimensions={1}, use_global_device_ids=true | all-gather | bytes 655360 | tf_op jit(solution)/shard_map/all_gather | solution.py:33
  64.1 0.6 convolution_negate_fusion
  64.7 0.7 dynamic-slice_bitcast_fusion
  65.4 72.5 %all-gather.2.cloned.1.call-done = f32[256,8192]{1,0:T(8,128)} async-done(((f32[32,8192]{1,0:T(8,128)}), f32[256,8192]{1,0:T(8,128)}) %all-gather.2.cloned.1.call-update) | async-done | bytes 8388624 | tf_op jit(solution)/shard_map/all_gather | solution.py:35
  137.9 9.4 %fusion.14 = f32[32,8192]{1,0:T(8,128)} fusion(f32[256,8192]{1,0:T(8,128)} %all-gather.2.cloned.1.call-done, f32[256,256]{1,0:T(8,128)S(1)} %convolution_multiply_fusion, s32[]{:T(128)S(6)} %select_n.27), kind=kOutput, calls=%fused_computation.30 | convolution fusion | flops 805306368 | bytes 9469956 | tf_op jit(solution)/shard_map/dot_general | solution.py:38
  147.3 0.0 copy-done
  147.3 18.8 %convolution_add_fusion = f32[512,8192]{1,0:T(8,128)} fusion(f32[512,8192]{1,0:T(8,128)} %param.7, f32[256,512]{1,0:T(8,128)S(1)} %convolution_negate_fusion, f32[256,8192]{1,0:T(8,128)S(1)} %copy-done), kind=kOutput, calls=%fused_computation.1 | convolution fusion | flops 12889096192 | bytes 42467328 | tf_op jit(solution)/shard_map/dot_general | solution.py:37
  (4 shorter events, 0.0 us)
Async XLA Ops:
  7.2 49.5 %copy-start.1 = (f32[512,64]{0,1:T(8,128)S(1)}, f32[512,64]{0,1:T(8,128)}, u32[]{:S(2)}) copy-start(f32[512,64]{0,1:T(8,128)} %param.4) | copy-start | bytes 393220
  7.2 130.7 %all-gather.2.cloned.1.call-start = ((), (), s32[]{:S(2)}) async-start(), calls=%async_computation | async-start | bytes 9437184 | tf_op jit(solution)/shard_map/all_gather | solution.py:35
  137.9 9.4 %copy-start = (f32[256,8192]{1,0:T(8,128)S(1)}, f32[256,8192]{1,0:T(8,128)}, u32[]{:S(2)}) copy-start(f32[256,8192]{1,0:T(8,128)} %all-gather.2.cloned.1.call-done) | copy-start | bytes 25165828
Sparse Core Ops, SparseCore 0:
  10.1 127.7 all-gather.1
where the time goes:
time: 173 us
  waiting for transfers between devices  73.2 us (42%)
  blocking collectives  47 us (27%)
  matrix products  34.3 us (20%)
  between operations  14.2 us (8%)
  local copies, waits for them, and re-layouts  3.92 us (2%)
    all_gather x1, waiting for transfers between devices, shards(): piece = lax.all_gather(row_panel, 'mc', axis=0, tiled=True)  72.5 us
    all_gather x1, blocking collectives, shards(): diag_part = lax.all_gather(diag_block, 'mc', axis=0, tiled=True)  33.8 us
    dot_general x1, matrix products, shards(): jnp.dot(column_whole, piece, precision=lax.Precision.HIGHEST)  18.8 us
    dot_general x1, matrix products, shards(): scaled_sum = jnp.dot(own_inverse, piece, precision=lax.Precision.HIGHEST)  9.35 us
    all_gather x1, blocking collectives, shards(): gathered = lax.all_gather(column_panel, 'mr', axis=1, tiled=True)  7.45 us
    all_gather x1, blocking collectives, shards(): diag_whole = lax.all_gather(diag_part, 'mr', axis=1, tiled=True)  5.78 us
  transfers between devices with their start and end apart: 1, of which 1 were waited for; matrix products, arithmetic and copies ran while one was open for 6% of the time, Pallas kernels for 0%

commit v1 on v0

v1 whole, which is shorter than its diff:
```python
import functools

import jax
import jax.numpy as jnp
from jax import lax
from jax.experimental import pallas as pl
from jax.experimental.pallas import tpu as pltpu
from jax.sharding import PartitionSpec as P

HIGHEST = lax.Precision.HIGHEST


def dot(a, b):
    return jnp.dot(a, b, precision=HIGHEST, preferred_element_type=jnp.float32)


def upper_inverse(matrix):
    order = matrix.shape[0]
    row = lax.broadcasted_iota(jnp.int32, (order, order), 0)
    col = lax.broadcasted_iota(jnp.int32, (order, order), 1)
    on_diag = row == col
    pivots = jnp.where(on_diag, matrix, 0.0)
    recip_col = 1.0 / jnp.sum(pivots, axis=1, keepdims=True)
    recip_row = 1.0 / jnp.sum(pivots, axis=0, keepdims=True)
    power = -(recip_col * jnp.where(col > row, matrix, 0.0))
    identity = jnp.where(on_diag, 1.0, 0.0)
    product = identity + power
    steps = max((order - 1).bit_length(), 1)
    for level in range(steps - 1):
        power = dot(power, power)
        product = dot(product, identity + power)
    return product * recip_row


def split(value):
    high = value.astype(jnp.bfloat16)
    low = (value - high.astype(jnp.float32)).astype(jnp.bfloat16)
    return high, low


def kernel(n_mc, n_mr, chunks, tile,
           column_ref, diag_ref, row_ref, trailing_ref,
           solved_ref, inverse_ref, scaled_ref, updated_ref,
           panel, columns, diags, matrix, flipped, left_high, left_low,
           load_sem, trail_sem, send_sem, recv_sem,
           diag_send, diag_recv, block_send, block_recv, col_send, col_recv):
    mc = lax.axis_index("mc")
    mr = lax.axis_index("mr")
    levels = n_mc // 2
    z = mc // 2
    x = lax.rem(mc, 2)
    rows = row_ref.shape[0]
    half = rows // 2
    cols = row_ref.shape[1]
    width = cols // chunks
    block_cols = diag_ref.shape[1]
    height = column_ref.shape[1]

    def at(mc_index, mr_index):
        return {"mc": mc_index, "mr": mr_index}

    own_row = pltpu.make_async_copy(
        row_ref, panel.at[pl.ds(pl.multiple_of(mc * rows, rows), rows)], load_sem.at[0])
    own_diag = pltpu.make_async_copy(
        diag_ref, diags.at[mr, pl.ds(pl.multiple_of(mc * rows, rows), rows)], load_sem.at[1])
    own_part = lambda k: pl.ds(pl.multiple_of(k * block_cols, block_cols), block_cols)
    own_column = pltpu.make_async_copy(column_ref, columns.at[own_part(mr)], load_sem.at[2])
    own_row.start()
    own_diag.start()
    own_column.start()

    barrier = pltpu.get_barrier_semaphore()
    for step in range(1, n_mc):
        pl.semaphore_signal(barrier, inc=1, device_id=at(lax.rem(mc + step, n_mc), mr),
                            device_id_type=pl.DeviceIdType.MESH)
    for step in range(1, n_mr):
        pl.semaphore_signal(barrier, inc=1, device_id=at(mc, lax.rem(mr + step, n_mr)),
                            device_id_type=pl.DeviceIdType.MESH)
    pl.semaphore_wait(barrier, n_mc + n_mr - 2)

    def piece(shard, c, low=None):
        first = pl.multiple_of(shard * rows, rows)
        count = rows
        if low is not None:
            first = pl.multiple_of(shard * rows + low * half, half)
            count = half
        return panel.at[pl.ds(first, count), pl.ds(pl.multiple_of(c * width, width), width)]

    def copy(shard, c, way, slot, target, low=None):
        ref = piece(shard, c, low)
        return pltpu.make_async_remote_copy(
            src_ref=ref, dst_ref=ref,
            send_sem=send_sem.at[way, slot, c],
            recv_sem=recv_sem.at[2 * shard + (1 if low == 1 else 0), c],
            device_id=at(target, mr), device_id_type=pl.DeviceIdType.MESH)

    down = jnp.maximum(mc - 2, 0)
    up = jnp.minimum(mc + 2, n_mc - 1)
    across = z * 2 + 1 - x

    def diag_copy(step, source, target):
        ref = diags.at[mr, pl.ds(pl.multiple_of(source * rows, rows), rows)]
        return pltpu.make_async_remote_copy(
            src_ref=ref, dst_ref=ref, send_sem=diag_send.at[step], recv_sem=diag_recv.at[step],
            device_id=at(target, mr), device_id_type=pl.DeviceIdType.MESH)

    def block_copy(step, source, target):
        ref = diags.at[source]
        return pltpu.make_async_remote_copy(
            src_ref=ref, dst_ref=ref, send_sem=block_send.at[step], recv_sem=block_recv.at[step],
            device_id=at(mc, target), device_id_type=pl.DeviceIdType.MESH)

    def column_copy(step, source, target):
        ref = columns.at[own_part(source)]
        return pltpu.make_async_remote_copy(
            src_ref=ref, dst_ref=ref, send_sem=col_send.at[step], recv_sem=col_recv.at[step],
            device_id=at(mc, target), device_id_type=pl.DeviceIdType.MESH)

    own_diag.wait()
    for step in range(1, n_mc):
        diag_copy(step, mc, lax.rem(mc + step, n_mc)).start()
    own_row.wait()

    @pl.loop(0, chunks)
    def _(c):
        @pl.when(z > 0)
        def _():
            copy(mc, c, 0, z, down).start()

        @pl.when(z < levels - 1)
        def _():
            copy(mc, c, 1, z, up).start()

        copy(mc, c, 2, z, across).start()

    own_column.wait()
    for step in range(1, n_mr):
        column_copy(step, mr, lax.rem(mr + step, n_mr)).start()

    def trail_copy(c):
        part = pl.ds(pl.multiple_of(c * width, width), width)
        return pltpu.make_async_copy(trailing_ref.at[:, part], updated_ref.at[:, part], trail_sem.at[c])

    @pl.loop(0, chunks)
    def _(c):
        trail_copy(c).start()

    for step in range(1, n_mc):
        diag_copy(step, lax.rem(mc + n_mc - step, n_mc), lax.rem(mc + step, n_mc)).wait_recv()
    for step in range(1, n_mr):
        block_copy(step, mr, lax.rem(mr + step, n_mr)).start()
    for step in range(1, n_mr):
        block_copy(step, lax.rem(mr + n_mr - step, n_mr), lax.rem(mr + step, n_mr)).wait_recv()
    for k in range(n_mr):
        matrix[:, k * block_cols:(k + 1) * block_cols] = diags[k]
    matrix[...] = upper_inverse(matrix[...])
    own_inverse = matrix[pl.ds(pl.multiple_of(mc * rows, rows), rows), :]
    for step in range(1, n_mr):
        column_copy(step, lax.rem(mr + n_mr - step, n_mr), lax.rem(mr + step, n_mr)).wait_recv()
    flipped[...] = -lax.dot_general(
        matrix[...], columns[...], (((0,), (0,)), ((), ())),
        precision=HIGHEST, preferred_element_type=jnp.float32)
    solved_ref[...] = flipped[own_part(mr), :]
    left_high[0:height, :], left_low[0:height, :] = split(flipped[...].T)
    left_high[height:height + rows, :], left_low[height:height + rows, :] = split(own_inverse)
    for k in range(n_mr):
        @pl.when(mr == k)
        def _():
            inverse_ref[...] = own_inverse[:, k * block_cols:(k + 1) * block_cols]

    first_half_only = lambda q: jnp.logical_or(
        jnp.logical_and(q == levels - 1, z != levels - 1), jnp.logical_and(q == 0, z != 0))

    def each_across(q, c, act):
        @pl.when(first_half_only(q))
        def _():
            act(copy(2 * q + x, c, 2, q, across, 0))

        @pl.when(jnp.logical_not(first_half_only(q)))
        def _():
            act(copy(2 * q + x, c, 2, q, across))

    start = lambda d: d.start()
    other = 1 - x
    top = 2 * (levels - 1) + other
    bottom = other

    for phase in range(levels - 1):
        above = z + 1 + phase
        below = z - 1 - phase

        @pl.loop(0, chunks)
        def _(c):
            @pl.when(above < levels)
            def _():
                copy(2 * above + x, c, 0, above, down).wait_recv()

                @pl.when(z > 0)
                def _():
                    copy(2 * above + x, c, 0, above, down).start()

                each_across(above, c, start)

            @pl.when(below >= 0)
            def _():
                copy(2 * below + x, c, 1, below, up).wait_recv()

                @pl.when(z < levels - 1)
                def _():
                    copy(2 * below + x, c, 1, below, up).start()

                each_across(below, c, start)

            if phase == 0:
                copy(2 * z + other, c, 2, z, across).wait_recv()

                @pl.when(z == levels - 1)
                def _():
                    copy(top, c, 0, levels, down, 1).start()

                @pl.when(z == 0)
                def _():
                    copy(bottom, c, 1, levels, up, 1).start()

            @pl.when(above == levels)
            def _():
                @pl.when(z < levels - 1)
                def _():
                    copy(top, c, 0, levels, down, 1).wait_recv()

                    @pl.when(z > 0)
                    def _():
                        copy(top, c, 0, levels, down, 1).start()

            @pl.when(below == -1)
            def _():
                @pl.when(z > 0)
                def _():
                    copy(bottom, c, 1, levels, up, 1).wait_recv()

                    @pl.when(z < levels - 1)
                    def _():
                        copy(bottom, c, 1, levels, up, 1).start()

    @pl.loop(0, chunks)
    def _(c):
        trail_copy(c).wait()

        @pl.when(z == 0)
        def _():
            copy(top, c, 0, levels, down, 1).wait_recv()

        @pl.when(z == levels - 1)
        def _():
            copy(bottom, c, 1, levels, up, 1).wait_recv()

        for q in range(levels):
            def receive(low):
                copy(2 * q + other, c, 2, q, across, low).wait_recv()

            @pl.when(jnp.logical_and(z != q, first_half_only(q)))
            def _():
                receive(0)

            @pl.when(jnp.logical_and(z != q, jnp.logical_not(first_half_only(q))))
            def _():
                receive(None)

        for t in range(width // tile):
            part = pl.ds(pl.multiple_of(c * width + t * tile, tile), tile)
            right_high, right_low = split(panel[:, part])
            product = jnp.dot(left_high[...], right_low, preferred_element_type=jnp.float32)
            product += jnp.dot(left_low[...], right_high, preferred_element_type=jnp.float32)
            product += jnp.dot(left_high[...], right_high, preferred_element_type=jnp.float32)
            updated_ref[:, part] = updated_ref[:, part] + product[0:height]
            scaled_ref[:, part] = product[height:height + rows]

    for step in range(1, n_mc):
        diag_copy(step, mc, lax.rem(mc + step, n_mc)).wait_send()
    for step in range(1, n_mr):
        block_copy(step, mr, lax.rem(mr + step, n_mr)).wait_send()
        column_copy(step, mr, lax.rem(mr + step, n_mr)).wait_send()

    @pl.loop(0, chunks)
    def _(c):
        for q in range(levels):
            @pl.when(jnp.logical_and(z > 0, z <= q))
            def _():
                copy(2 * q + x, c, 0, q, down).wait_send()

            @pl.when(jnp.logical_and(z < levels - 1, z >= q))
            def _():
                copy(2 * q + x, c, 1, q, up).wait_send()

            each_across(q, c, lambda d: d.wait_send())

        @pl.when(z > 0)
        def _():
            copy(top, c, 0, levels, down, 1).wait_send()

        @pl.when(z < levels - 1)
        def _():
            copy(bottom, c, 1, levels, up, 1).wait_send()


def store(*refs):
    n = len(refs) // 2
    copies = [pltpu.make_async_copy(refs[i], refs[n + i], refs[-1].at[i]) for i in range(n)]
    for c in copies:
        c.start()
    for c in copies:
        c.wait()


def shards(n_mc, n_mr, column_panel, diag_block, row_panel, trailing):
    rows, block_cols = diag_block.shape
    height, cols = trailing.shape
    order = rows * n_mc
    levels = n_mc // 2
    chunks = max(1, 32 // levels)
    while cols % (chunks * 128):
        chunks //= 2
    width = cols // chunks
    tile = 512 if width % 512 == 0 else 128
    dma = pltpu.SemaphoreType.DMA
    f32 = jnp.float32
    anywhere = pl.BlockSpec(memory_space=pl.ANY)
    vmem = pl.BlockSpec(memory_space=pltpu.VMEM)
    parts = pl.pallas_call(
        functools.partial(kernel, n_mc, n_mr, chunks, tile),
        out_shape=(
            pltpu.VMEM((block_cols, height), f32),
            pltpu.VMEM(diag_block.shape, f32),
            pltpu.VMEM(row_panel.shape, f32),
            pltpu.VMEM(trailing.shape, f32),
        ),
        in_specs=[pl.BlockSpec(memory_space=pltpu.HBM)] * 4,
        out_specs=(vmem,) * 4,
        scratch_shapes=[
            pltpu.VMEM((order, cols), f32),
            pltpu.VMEM((order, height), f32),
            pltpu.VMEM((n_mr, order, block_cols), f32),
            pltpu.VMEM((order, order), f32),
            pltpu.VMEM((order, height), f32),
            pltpu.VMEM((height + rows, order), jnp.bfloat16),
            pltpu.VMEM((height + rows, order), jnp.bfloat16),
            dma((3,)), dma((chunks,)),
            dma((3, levels + 1, chunks)), dma((2 * n_mc, chunks)),
            dma((n_mc,)), dma((n_mc,)), dma((n_mr,)), dma((n_mr,)), dma((n_mr,)), dma((n_mr,)),
        ],
        compiler_params=pltpu.CompilerParams(
            collective_id=0, has_side_effects=True, vmem_limit_bytes=26 * 1024 * 1024),
    )(column_panel.T, diag_block, row_panel, trailing)
    solved, inverse, scaled, updated = pl.pallas_call(
        store,
        out_shape=tuple(jax.ShapeDtypeStruct(part.shape, f32) for part in parts),
        in_specs=[vmem] * 4,
        out_specs=(anywhere,) * 4,
        scratch_shapes=[dma((4,))],
        compiler_params=pltpu.CompilerParams(vmem_limit_bytes=1024 * 1024),
    )(*parts)
    return solved.T, inverse, scaled, updated


def solution(mesh):
    placed = (P("mc", "mr"),) * 4
    return jax.shard_map(
        functools.partial(shards, mesh.shape["mc"], mesh.shape["mr"]),
        mesh=mesh, in_specs=placed, out_specs=placed, check_vma=False)
```

time: 173 us -> 102 us (0.59)
  Pallas kernels: 0 us -> 98.6 us
  waiting for transfers between devices: 73.2 us -> 0 us
  blocking collectives: 47 us -> 0 us
  matrix products: 34.3 us -> 0 us
  between operations: 14.2 us -> 0.65 us
    pallas_call x0 -> x2, Pallas kernels: none -> 98.6 us  [the longest x1 92 us: shards(): pl.pallas_call(functools.partial(kernel, n_mc, n_mr, chunks, tile), out_s...]
    all_gather x1 -> x0, waiting for transfers between devices: 72.5 us -> none  [shards(): piece = lax.all_gather(row_panel, 'mc', axis=0, tiled=True)]
    all_gather x3 -> x0, blocking collectives: 47 us -> none  [the longest x1 33.8 us: shards(): diag_part = lax.all_gather(diag_block, 'mc', axis=0, tiled=True)]
    dot_general x17 -> x0, matrix products: 34.3 us -> none  [the longest x1 18.8 us: shards(): jnp.dot(column_whole, piece, precision=lax.Precision.HIGHEST)]
    unnamed x4 -> x6, local copies, waits for them, and re-layouts: 0.01 us -> 2.84 us
    gather x1 -> x0, local copies, waits for them, and re-layouts: 2.34 us -> none  [upper_inverse(): pivots = jnp.diagonal(upper)]
  transfers between devices with their start and end apart: 1 -> 0, of which waited for: 1 -> 0; matrix products, arithmetic and copies ran while one was open for 6% -> 0% of each run, Pallas kernels for 0% -> 0%
where the time goes in v1:
time: 102 us
  Pallas kernels  98.6 us (97%)
  local copies, waits for them, and re-layouts  2.84 us (3%)
    pallas_call x1, Pallas kernels, shards(): pl.pallas_call(functools.partial(kernel, n_mc, n_mr, chunks, tile), out_s...  92 us
    pallas_call x1, Pallas kernels, shards(): pl.pallas_call(store, out_shape=tuple((jax.ShapeDtypeStruct(part.shape, f...  6.59 us
    unnamed x6, local copies, waits for them, and re-layouts  2.84 us

profile of v1, /device:TPU:0, one launch (start us, length us, event | category | flops | bytes accessed | tf_op | source)
XLA Modules:
  0.0 102.0 jit_solution(6914417512047905206)
XLA Ops:
  0.6 0.0 copy-start
  0.6 1.2 %copy-done = f32[32,8192]{1,0:T(8,128)S(1)} copy-done((f32[32,8192]{1,0:T(8,128)S(1)}, f32[32,8192]{1,0:T(8,128)}, u32[]{:S(2)}) %copy-start) | copy-done | bytes 1048600
  1.9 0.0 copy-start.1
  1.9 0.9 copy-done.1
  2.8 0.0 copy-start.2
  2.8 0.7 copy-done.2
  3.5 92.0 %shard_map.75 = (f32[64,512]{1,0:T(8,128)S(1)}, f32[32,64]{1,0:T(8,128)S(1)}, f32[32,8192]{1,0:T(8,128)S(1)}, f32[512,8192]{1,0:T(8,128)S(1)}) custom-call(f32[64,512]{1,0:T(8,128)S(1)} %bitcast.2, f32[32,64]{1,0:T(8,128)S(1)} %copy-done.2, f32[32,8192]{1,0:T(8,128)S(1)} %copy-done, f32[512,8192]{1,0:T(8,128)} %trailing_ref.1), custom_call_target="tpu_custom_call" | custom-call | tf_op jit(solution)/shard_map/pallas_call | solution.py:329
  95.5 6.6 %shard_map.76 = (f32[64,512]{1,0:T(8,128)}, f32[32,64]{1,0:T(8,128)}, f32[32,8192]{1,0:T(8,128)}, f32[512,8192]{1,0:T(8,128)}) custom-call(f32[64,512]{1,0:T(8,128)S(1)} %get-tuple-element.12.refs_0_, f32[32,64]{1,0:T(8,128)S(1)} %get-tuple-element.13.refs_1_, f32[32,8192]{1,0:T(8,128)S(1)} %get-tuple-element.14.refs_2_, ...), custom_call_target="tpu_custom_call" | custom-call | tf_op jit(solution)/shard_map/pallas_call | solution.py:354
Async XLA Ops:
  0.6 1.2 %copy-start = (f32[32,8192]{1,0:T(8,128)S(1)}, f32[32,8192]{1,0:T(8,128)}, u32[]{:S(2)}) copy-start(f32[32,8192]{1,0:T(8,128)} %row_ref.1) | copy-start | bytes 3145732
  1.9 0.9 copy-start.1
  2.8 0.7 copy-start.2

commit v2 on v1

--- a/solution.py
+++ b/solution.py
@@ -7,6 +7,7 @@
 from jax.experimental.pallas import tpu as pltpu
 from jax.sharding import PartitionSpec as P
 
+VMEM_BYTES = 67043328
 HIGHEST = lax.Precision.HIGHEST
 
 
@@ -116,22 +117,23 @@
             src_ref=ref, dst_ref=ref, send_sem=col_send.at[step], recv_sem=col_recv.at[step],
             device_id=at(mc, target), device_id_type=pl.DeviceIdType.MESH)
 
+    own_row.wait()
+
+    @pl.loop(0, chunks)
+    def _(c):
+        @pl.when(z > 0)
+        def _():
+            copy(mc, c, 0, z, down).start()
+
+        @pl.when(z < levels - 1)
+        def _():
+            copy(mc, c, 1, z, up).start()
+
+        copy(mc, c, 2, z, across).start()
+
     own_diag.wait()
     for step in range(1, n_mc):
         diag_copy(step, mc, lax.rem(mc + step, n_mc)).start()
-    own_row.wait()
-
-    @pl.loop(0, chunks)
-    def _(c):
-        @pl.when(z > 0)
-        def _():
-            copy(mc, c, 0, z, down).start()
-
-        @pl.when(z < levels - 1)
-        def _():
-            copy(mc, c, 1, z, up).start()
-
-        copy(mc, c, 2, z, across).start()
 
     own_column.wait()
     for step in range(1, n_mr):
@@ -144,29 +146,6 @@
     @pl.loop(0, chunks)
     def _(c):
         trail_copy(c).start()
-
-    for step in range(1, n_mc):
-        diag_copy(step, lax.rem(mc + n_mc - step, n_mc), lax.rem(mc + step, n_mc)).wait_recv()
-    for step in range(1, n_mr):
-        block_copy(step, mr, lax.rem(mr + step, n_mr)).start()
-    for step in range(1, n_mr):
-        block_copy(step, lax.rem(mr + n_mr - step, n_mr), lax.rem(mr + step, n_mr)).wait_recv()
-    for k in range(n_mr):
-        matrix[:, k * block_cols:(k + 1) * block_cols] = diags[k]
-    matrix[...] = upper_inverse(matrix[...])
-    own_inverse = matrix[pl.ds(pl.multiple_of(mc * rows, rows), rows), :]
-    for step in range(1, n_mr):
-        column_copy(step, lax.rem(mr + n_mr - step, n_mr), lax.rem(mr + step, n_mr)).wait_recv()
-    flipped[...] = -lax.dot_general(
-        matrix[...], columns[...], (((0,), (0,)), ((), ())),
-        precision=HIGHEST, preferred_element_type=jnp.float32)
-    solved_ref[...] = flipped[own_part(mr), :]
-    left_high[0:height, :], left_low[0:height, :] = split(flipped[...].T)
-    left_high[height:height + rows, :], left_low[height:height + rows, :] = split(own_inverse)
-    for k in range(n_mr):
-        @pl.when(mr == k)
-        def _():
-            inverse_ref[...] = own_inverse[:, k * block_cols:(k + 1) * block_cols]
 
     first_half_only = lambda q: jnp.logical_or(
         jnp.logical_and(q == levels - 1, z != levels - 1), jnp.logical_and(q == 0, z != 0))
@@ -185,7 +164,34 @@
     top = 2 * (levels - 1) + other
     bottom = other
 
+    def invert():
+        for step in range(1, n_mc):
+            diag_copy(step, lax.rem(mc + n_mc - step, n_mc), lax.rem(mc + step, n_mc)).wait_recv()
+        for step in range(1, n_mr):
+            block_copy(step, mr, lax.rem(mr + step, n_mr)).start()
+        for step in range(1, n_mr):
+            block_copy(step, lax.rem(mr + n_mr - step, n_mr), lax.rem(mr + step, n_mr)).wait_recv()
+        for k in range(n_mr):
+            matrix[:, k * block_cols:(k + 1) * block_cols] = diags[k]
+        matrix[...] = upper_inverse(matrix[...])
+        own_inverse = matrix[pl.ds(pl.multiple_of(mc * rows, rows), rows), :]
+        for step in range(1, n_mr):
+            column_copy(step, lax.rem(mr + n_mr - step, n_mr), lax.rem(mr + step, n_mr)).wait_recv()
+        flipped[...] = -lax.dot_general(
+            matrix[...], columns[...], (((0,), (0,)), ((), ())),
+            precision=HIGHEST, preferred_element_type=jnp.float32)
+        solved_ref[...] = flipped[own_part(mr), :]
+        left_high[0:height, :], left_low[0:height, :] = split(flipped[...].T)
+        left_high[height:height + rows, :], left_low[height:height + rows, :] = split(own_inverse)
+        for k in range(n_mr):
+            @pl.when(mr == k)
+            def _():
+                inverse_ref[...] = own_inverse[:, k * block_cols:(k + 1) * block_cols]
+
     for phase in range(levels - 1):
+        if phase == min(1, levels - 2):
+            invert()
+
         above = z + 1 + phase
         below = z - 1 - phase
 
@@ -304,8 +310,15 @@
 
 
 def store(*refs):
-    n = len(refs) // 2
-    copies = [pltpu.make_async_copy(refs[i], refs[n + i], refs[-1].at[i]) for i in range(n)]
+    sources, targets, sem = refs[:4], refs[4:8], refs[8]
+    strips = sem.shape[0] - 3
+    deep = sources[3].shape[0] // strips
+    copies = []
+    for i in range(strips):
+        part = pl.ds(i * deep, deep)
+        copies.append(pltpu.make_async_copy(sources[3].at[part], targets[3].at[part], sem.at[3 + i]))
+    for i in range(3):
+        copies.append(pltpu.make_async_copy(sources[i], targets[i], sem.at[i]))
     for c in copies:
         c.start()
     for c in copies:
@@ -317,11 +330,12 @@
     height, cols = trailing.shape
     order = rows * n_mc
     levels = n_mc // 2
-    chunks = max(1, 32 // levels)
+    chunks = max(1, 16 // levels)
     while cols % (chunks * 128):
         chunks //= 2
     width = cols // chunks
     tile = 512 if width % 512 == 0 else 128
+    held = 4 * (height * cols + rows * cols + block_cols * height + rows * 128) + 64 * 1024
     dma = pltpu.SemaphoreType.DMA
     f32 = jnp.float32
     anywhere = pl.BlockSpec(memory_space=pl.ANY)
@@ -349,14 +363,14 @@
             dma((n_mc,)), dma((n_mc,)), dma((n_mr,)), dma((n_mr,)), dma((n_mr,)), dma((n_mr,)),
         ],
         compiler_params=pltpu.CompilerParams(
-            collective_id=0, has_side_effects=True, vmem_limit_bytes=26 * 1024 * 1024),
+            collective_id=0, has_side_effects=True, vmem_limit_bytes=VMEM_BYTES - held),
     )(column_panel.T, diag_block, row_panel, trailing)
     solved, inverse, scaled, updated = pl.pallas_call(
         store,
         out_shape=tuple(jax.ShapeDtypeStruct(part.shape, f32) for part in parts),
         in_specs=[vmem] * 4,
         out_specs=(anywhere,) * 4,
-        scratch_shapes=[dma((4,))],
+        scratch_shapes=[dma((3 + 8,))],
         compiler_params=pltpu.CompilerParams(vmem_limit_bytes=1024 * 1024),
     )(*parts)
     return solved.T, inverse, scaled, updated

time: 102 us -> 98.6 us (0.967)
  local copies, waits for them, and re-layouts: 2.84 us -> 0 us
    unnamed x6 -> x0, local copies, waits for them, and re-layouts: 2.84 us -> none
where the time goes in v2:
time: 98.6 us; the launch traced here: 98.4 us
  Pallas kernels  97.8 us (99%)
    pallas_call x1, Pallas kernels, shards(): pl.pallas_call(functools.partial(kernel, n_mc, n_mr, chunks, tile), out_s...  91.5 us
    pallas_call x1, Pallas kernels, shards(): pl.pallas_call(store, out_shape=tuple((jax.ShapeDtypeStruct(part.shape, f...  6.28 us

profile of v2, /device:TPU:0, one launch (start us, length us, event | category | flops | bytes accessed | tf_op | source)
XLA Modules:
  0.0 98.4 jit_solution(8846483247581796132)
XLA Ops:
  0.6 91.5 %shard_map.75 = (f32[64,512]{1,0:T(8,128)S(1)}, f32[32,64]{1,0:T(8,128)S(1)}, f32[32,8192]{1,0:T(8,128)S(1)}, f32[512,8192]{1,0:T(8,128)S(1)}) custom-call(f32[64,512]{1,0:T(8,128)} %bitcast.2, f32[32,64]{1,0:T(8,128)} %diag_ref.1, f32[32,8192]{1,0:T(8,128)} %row_ref.1, f32[512,8192]{1,0:T(8,128)} %trailing_ref.1), custom_call_target="tpu_custom_call" | custom-call | tf_op jit(solution)/shard_map/pallas_call | solution.py:343
  92.2 6.3 %shard_map.76 = (f32[64,512]{1,0:T(8,128)}, f32[32,64]{1,0:T(8,128)}, f32[32,8192]{1,0:T(8,128)}, f32[512,8192]{1,0:T(8,128)}) custom-call(f32[64,512]{1,0:T(8,128)S(1)} %get-tuple-element.12.refs_0_, f32[32,64]{1,0:T(8,128)S(1)} %get-tuple-element.13.refs_1_, f32[32,8192]{1,0:T(8,128)S(1)} %get-tuple-element.14.refs_2_, ...), custom_call_target="tpu_custom_call" | custom-call | tf_op jit(solution)/shard_map/pallas_call | solution.py:368
